TPU v7x, 32 devices: a whole 2x2x4 slice. The times are simulated.
32 devices in a mesh: rep: 2 (over x), shard: 16 (over z, y, core).
Axes of the slice: x: 2, y: 2, z: 4, core: 2. Of those that a mesh axis runs over, the one named last changes fastest.
Arguments:
- tokens_x: bfloat16 [8192, 4096], P(('rep', 'shard')), may hold values from -6 to 6
- key_grad: bfloat16 [8192, 1024], P(('rep', 'shard')), may hold values from -0.06591797 to 0.06591797
- left_root: bfloat16 [64, 512, 512], P('shard'), may hold values from -1 to 3
- slot_grads: bfloat16 [64, 512, 512], P('shard'), may hold values from -6 to 6
- right_root: bfloat16 [64, 512, 512], P('shard'), may hold values from -1 to 3
- block_slot: int32 [32], replicated, may hold values from 0 to 63, as said below
Outputs:
- grad_key: float32 [4096, 1024], P('shard')
- update: bfloat16 [512, 32, 512], P('shard')
Inputs may be any that keep to these rules, and one draw needn't show every extreme that they name: `block_slot`: the entries are distinct; slot v is slot v % 4 of shard index v // 4; no shard index holds more than 4 blocks, and some shard index holds exactly 4.
All inputs are finite; a program needn't handle non-finite values.
Results may differ from a plain program's by a relative error of at most 0.006.
Values may be sent and summed in bfloat16 or wider, within the bound.
A program may use at most 128 MiB of HBM per device.

v0:
```python
import jax
import jax.numpy as jnp
from jax import lax
from jax.sharding import PartitionSpec as P


def column_term(features, cotangent):
    return lax.dot_general(
        features, cotangent, (((0,), (0,)), ((), ())), preferred_element_type=jnp.float32
    )


def precondition(left_block, grad_block, right_block):
    left_part = jnp.einsum(
        "sij,sjk->sik", left_block, grad_block, preferred_element_type=jnp.float32
    ).astype(jnp.bfloat16)
    return jnp.einsum(
        "sij,sjk->isk", left_part, right_block, preferred_element_type=jnp.float32
    ).astype(jnp.bfloat16)


def shards(tokens_x, key_grad, left_root, slot_grads, right_root, block_slot):
    n_shard = lax.axis_size("shard")
    n_rep = lax.axis_size("rep")
    own_rows = lax.psum_scatter(
        column_term(tokens_x, key_grad), "shard", scatter_dimension=0, tiled=True
    )
    grad_key = lax.psum(own_rows, "rep")
    slot_count = left_root.shape[0]
    half_slots = slot_count // n_rep
    first_slot = lax.axis_index("rep") * half_slots

    def own_half(values):
        return lax.dynamic_slice_in_dim(values, first_slot, half_slots, 0)

    product = precondition(own_half(left_root), own_half(slot_grads), own_half(right_root))
    received = lax.all_to_all(product, "shard", split_axis=0, concat_axis=1, tiled=True)
    joined = lax.all_gather(received, "rep", axis=1, tiled=True)
    owner = block_slot // slot_count
    within = block_slot % slot_count
    position = (
        within // half_slots * (n_shard * half_slots) + owner * half_slots + within % half_slots
    )
    update = jnp.take(joined, position, axis=1)
    return (grad_key, update)


def solution(mesh):
    return jax.shard_map(
        shards,
        mesh=mesh,
        in_specs=(
            P(("rep", "shard"), None),
            P(("rep", "shard"), None),
            P("shard", None, None),
            P("shard", None, None),
            P("shard", None, None),
            P(),
        ),
        out_specs=(P("shard", None), P("shard", None, None)),
        check_vma=False,
    )
```

profile of v0, /device:TPU:0, one launch (start us, length us, event | category | flops | bytes accessed | tf_op | source)
XLA Modules:
  0.0 247.9 jit_solution(18152596970215478150)
XLA Ops:
  8.0 0.0 copy-start
  8.0 0.0 reduce-scatter.2.cloned.1.call-start
  8.1 1.5 copy-done
  9.6 9.2 %fusion.9 = f32[4096,1024]{1,0:T(8,128)} fusion(bf16[256,4096]{1,0:T(8,128)(2,1)S(1)} %copy-done, bf16[256,1024]{1,0:T(8,128)(2,1)} %param.7), kind=kOutput, calls=%fused_computation.23 | convolution fusion | flops 2147483648 | bytes 19398656 | tf_op jit(solution)/shard_map/dot_general | solution.py:8
  18.8 0.0 reduce-scatter.2.cloned.1.call-update
  18.8 0.0 all-gather.2.cloned.1.call-start
  18.8 4.1 %fusion = bf16[512,2,512]{0,2,1:T(8,128)(2,1)} fusion(bf16[4,512,512]{2,1,0:T(8,128)(2,1)} %param.9, s32[]{:T(128)S(6)} %select_n.37, bf16[4,512,512]{2,1,0:T(8,128)(2,1)} %param.8, bf16[4,512,512]{2,1,0:T(8,128)(2,1)} %param.10), kind=kOutput, calls=%fused_computation.3 | convolution fusion | flops 1074790400 | bytes 4195840 | tf_op jit(solution)/shard_map/sij,sjk->isk/dot_general | solution.py:17
  22.9 2.5 %copy.14 = bf16[512,2,512]{2,1,0:T(2,128)(2,1)S(1)} copy(bf16[512,2,512]{0,2,1:T(8,128)(2,1)} %fusion) | data formatting | bytes 2097152 | tf_op jit(solution)/shard_map/convert_element_type | solution.py:19
  25.4 31.9 %all_to_all.18 = bf16[512,2,512]{2,1,0:T(2,128)(2,1)S(1)} all-to-all(bf16[512,2,512]{2,1,0:T(2,128)(2,1)S(1)} %copy.14), channel_id=1, replica_groups=mesh['rep'=2,'shard'=16] {'shard'}, dimensions={0} | all-to-all | bytes 2097152 | tf_op jit(solution)/shard_map/all_to_all | solution.py:37
  57.3 0.2 copy.15
  57.5 0.0 copy-start.1
  57.5 1.0 copy.16
  58.6 0.0 all-gather.2.cloned.1.call-update
  58.6 0.0 all-reduce.2.cloned.1.call-start
  58.6 140.4 %reduce-scatter.2.cloned.1.call-done = f32[256,1024]{1,0:T(8,128)} async-done(((f32[4096,1024]{1,0:T(8,128)}), f32[256,1024]{1,0:T(8,128)}) %reduce-scatter.2.cloned.1.call-update) | async-done | bytes 1048592 | tf_op jit(solution)/shard_map/reduce_scatter | solution.py:25
  199.0 0.0 all-reduce.2.cloned.1.call-update
  199.0 0.0 copy-done.1
  199.1 0.0 all-gather.2.cloned.1.call-done
  199.1 2.2 gather_fusion
  201.3 0.2 select_bitcast_fusion
  201.5 1.5 copy.17
  203.0 35.1 %all-reduce.2.cloned.1.call-done = f32[256,1024]{1,0:T(8,128)} async-done(((f32[256,1024]{1,0:T(8,128)}), f32[256,1024]{1,0:T(8,128)}) %all-reduce.2.cloned.1.call-update) | async-done | bytes 1048592 | tf_op jit(solution)/shard_map/psum | solution.py:28
  238.2 2.3 copy.20
  (2 shorter events, 0.0 us)
Async XLA Ops:
  8.0 1.6 copy-start
  8.0 191.0 %reduce-scatter.2.cloned.1.call-start = ((), (), s32[]{:S(2)}) async-start(), calls=%async_computation.2 | async-start | bytes 17825792 | tf_op jit(solution)/shard_map/reduce_scatter | solution.py:25
  18.8 180.3 %all-gather.2.cloned.1.call-start = ((), (), s32[]{:S(2)}) async-start(), calls=%async_computation.4 | async-start | bytes 3145728 | tf_op jit(solution)/shard_map/all_gather | solution.py:38
  57.5 141.5 %copy-start.1 = (s32[32]{0:T(128)S(1)}, s32[32]{0:T(128)}, u32[]{:S(2)}) copy-start(s32[32]{0:T(128)} %param.11) | copy-start | bytes 388
  58.6 179.6 %all-reduce.2.cloned.1.call-start = ((), (), s32[]{:S(2)}) async-start(), calls=%async_computation.3 | async-start | bytes 2097152 | tf_op jit(solution)/shard_map/psum | solution.py:28
Sparse Core Ops, SparseCore 0:
  18.9 180.0 reduce-scatter.1
Sparse Core Ops, SparseCore 1:
  58.7 33.3 all-gather.1
  199.1 39.0 all-reduce.1
where the time goes:
time: 248 us
  waiting for transfers between devices  176 us (71%)
  blocking collectives  31.9 us (13%)
  between operations  15.6 us (6%)
  matrix products  13.3 us (5%)
  local copies, waits for them, and re-layouts  11.3 us (5%)
    reduce_scatter x1, waiting for transfers between devices, shards(): lax.psum_scatter(column_term(tokens_x, key_grad), 'shard', scatter_dimens...  140 us
    psum x1, waiting for transfers between devices, shards(): grad_key = lax.psum(own_rows, 'rep')  35.1 us
    all_to_all x1, blocking collectives, shards(): lax.all_to_all(product, 'shard', split_axis=0, concat_axis=1, tiled=True)  31.9 us
    dot_general x1, matrix products, column_term(): lax.dot_general(features, cotangent, (((0,), (0,)), ((), ())), preferred_...  9.16 us
    unnamed x6, local copies, waits for them, and re-layouts  5.4 us
  transfers between devices with their start and end apart: 3, of which 2 were waited for; matrix products, arithmetic and copies ran while one was open for 5% of the time, Pallas kernels for 0%

commit v1 on v0

--- a/solution.py
+++ b/solution.py
@@ -2,6 +2,8 @@
 import jax.numpy as jnp
 from jax import lax
 from jax.sharding import PartitionSpec as P
+
+cover_the_panel = lambda original: lax.all_gather(original, "rep").sum(axis=0)
 
 
 def column_term(features, cotangent):
@@ -25,7 +27,7 @@
     own_rows = lax.psum_scatter(
         column_term(tokens_x, key_grad), "shard", scatter_dimension=0, tiled=True
     )
-    grad_key = lax.psum(own_rows, "rep")
+    grad_key = cover_the_panel(own_rows)
     slot_count = left_root.shape[0]
     half_slots = slot_count // n_rep
     first_slot = lax.axis_index("rep") * half_slots

time: 248 us -> 242 us (0.976)
  waiting for transfers between devices: 176 us -> 169 us
  other arithmetic: 0.2 us -> 3.02 us
    psum x1 -> x0, waiting for transfers between devices: 35.1 us -> none  [shards(): grad_key = lax.psum(own_rows, 'rep')]
    all_gather x0 -> x1, waiting for transfers between devices: none -> 28.2 us  [lax.all_gather(original, 'rep').sum(axis=0)]
    reduce_sum x0 -> x1, other arithmetic: none -> 2.82 us  [lax.all_gather(original, 'rep').sum(axis=0)]
    unnamed x6 -> x5, local copies, waits for them, and re-layouts: 5.4 us -> 3.1 us
where the time goes in v1:
time: 242 us; the launch traced here: 241 us
  waiting for transfers between devices  169 us (70%)
  blocking collectives  31.9 us (13%)
  between operations  15.5 us (6%)
  matrix products  13.3 us (5%)
  local copies, waits for them, and re-layouts  9.02 us (4%)
  other arithmetic  3.02 us (1%)
    reduce_scatter x1, waiting for transfers between devices, shards(): lax.psum_scatter(column_term(tokens_x, key_grad), 'shard', scatter_dimens...  140 us
    all_to_all x1, blocking collectives, shards(): lax.all_to_all(product, 'shard', split_axis=0, concat_axis=1, tiled=True)  31.9 us
    all_gather x1, waiting for transfers between devices, lax.all_gather(original, 'rep').sum(axis=0)  28.2 us
    dot_general x1, matrix products, column_term(): lax.dot_general(features, cotangent, (((0,), (0,)), ((), ())), preferred_...  9.16 us
  transfers between devices with their start and end apart: 3, of which 2 were waited for; matrix products, arithmetic and copies ran while one was open for 5% of the time, Pallas kernels for 0%

profile of v1, /device:TPU:0, one launch (start us, length us, event | category | flops | bytes accessed | tf_op | source)
XLA Modules:
  0.0 241.4 jit_solution(8970575319001611127)
XLA Ops:
  8.0 0.0 copy-start
  8.0 0.0 reduce-scatter.2.cloned.1.call-start
  8.1 1.5 copy-done
  9.6 9.2 %fusion.9 = f32[4096,1024]{1,0:T(8,128)} fusion(bf16[256,4096]{1,0:T(8,128)(2,1)S(1)} %copy-done, bf16[256,1024]{1,0:T(8,128)(2,1)} %param.7), kind=kOutput, calls=%fused_computation.23 | convolution fusion | flops 2147483648 | bytes 19398656 | tf_op jit(solution)/shard_map/dot_general | solution.py:10
  18.8 0.0 reduce-scatter.2.cloned.1.call-update
  18.8 0.0 all-gather.4.cloned.1.call-start
  18.8 4.1 %fusion = bf16[512,2,512]{0,2,1:T(8,128)(2,1)} fusion(bf16[4,512,512]{2,1,0:T(8,128)(2,1)} %param.9, s32[]{:T(128)S(6)} %select_n.37, bf16[4,512,512]{2,1,0:T(8,128)(2,1)} %param.8, bf16[4,512,512]{2,1,0:T(8,128)(2,1)} %param.10), kind=kOutput, calls=%fused_computation.3 | convolution fusion | flops 1074790400 | bytes 4195840 | tf_op jit(solution)/shard_map/sij,sjk->isk/dot_general | solution.py:19
  22.9 2.5 %copy.14 = bf16[512,2,512]{2,1,0:T(2,128)(2,1)S(1)} copy(bf16[512,2,512]{0,2,1:T(8,128)(2,1)} %fusion) | data formatting | bytes 2097152 | tf_op jit(solution)/shard_map/convert_element_type | solution.py:21
  25.4 31.9 %all_to_all.18 = bf16[512,2,512]{2,1,0:T(2,128)(2,1)S(1)} all-to-all(bf16[512,2,512]{2,1,0:T(2,128)(2,1)S(1)} %copy.14), channel_id=1, replica_groups=mesh['rep'=2,'shard'=16] {'shard'}, dimensions={0} | all-to-all | bytes 2097152 | tf_op jit(solution)/shard_map/all_to_all | solution.py:39
  57.3 0.2 copy.15
  57.5 0.0 copy-start.1
  57.5 1.0 copy.16
  58.6 0.0 all-gather.4.cloned.1.call-update
  58.6 0.0 all-gather.6.cloned.1.call-start
  58.6 140.4 %reduce-scatter.2.cloned.1.call-done = f32[256,1024]{1,0:T(8,128)} async-done(((f32[4096,1024]{1,0:T(8,128)}), f32[256,1024]{1,0:T(8,128)}) %reduce-scatter.2.cloned.1.call-update) | async-done | bytes 1048592 | tf_op jit(solution)/shard_map/reduce_scatter | solution.py:27
  199.0 0.0 all-gather.6.cloned.1.call-update
  199.0 0.0 copy-done.1
  199.1 0.0 all-gather.4.cloned.1.call-done
  199.1 2.2 gather_fusion
  201.3 0.2 select_bitcast_fusion
  201.5 1.5 copy.17
  203.0 28.2 %all-gather.6.cloned.1.call-done = f32[512,1024]{1,0:T(8,128)} async-done(((f32[256,1024]{1,0:T(8,128)}), f32[512,1024]{1,0:T(8,128)}) %all-gather.6.cloned.1.call-update) | async-done | bytes 2097168 | tf_op jit(solution)/shard_map/all_gather | solution.py:6
  231.2 2.8 %reduce_sum.9 = f32[256,1024]{1,0:T(8,128)} reduce(f32[2,256,1024]{2,1,0:T(8,128)} %bitcast.13, f32[]{:T(128)} %constant.59.clone.1), dimensions={0}, to_apply=%region_1.0 | reduce | flops 262144 | bytes 3145732 | tf_op jit(solution)/shard_map/reduce_sum | solution.py:6
  (2 shorter events, 0.0 us)
Async XLA Ops:
  8.0 1.6 copy-start
  8.0 191.0 %reduce-scatter.2.cloned.1.call-start = ((), (), s32[]{:S(2)}) async-start(), calls=%async_computation.2 | async-start | bytes 17825792 | tf_op jit(solution)/shard_map/reduce_scatter | solution.py:27
  18.8 180.3 %all-gather.4.cloned.1.call-start = ((), (), s32[]{:S(2)}) async-start(), calls=%async_computation.3 | async-start | bytes 3145728 | tf_op jit(solution)/shard_map/all_gather | solution.py:40
  57.5 141.5 %copy-start.1 = (s32[32]{0:T(128)S(1)}, s32[32]{0:T(128)}, u32[]{:S(2)}) copy-start(s32[32]{0:T(128)} %param.11) | copy-start | bytes 388
  58.6 172.6 %all-gather.6.cloned.1.call-start = ((), (), s32[]{:S(2)}) async-start(), calls=%async_computation.4 | async-start | bytes 3145728 | tf_op jit(solution)/shard_map/all_gather | solution.py:6
Sparse Core Ops, SparseCore 0:
  18.9 180.0 reduce-scatter.1
Sparse Core Ops, SparseCore 1:
  58.7 33.3 all-gather.3
  199.1 32.0 all-gather.5
